TPU v7x, 32 devices: a whole 2x2x4 slice. The times are simulated.
32 devices in a mesh: dp: 2 (over x), sp: 16 (over y, z, core).
Axes of the slice: x: 2, y: 2, z: 4, core: 2. Of those that a mesh axis runs over, the one named last changes fastest.
Arguments:
- q: bfloat16 [64, 32, 80], P('dp'), parts along dimension 0
- k: bfloat16 [64, 4096, 32, 80], P('dp', 'sp'), parts along dimension 0
- v: bfloat16 [64, 4096, 32, 80], P('dp', 'sp'), parts along dimension 0
Outputs:
- q: bfloat16 [64, 32, 80], P('dp'), parts along dimension 0
There are 2 independent parts. A program takes and returns all parts, laid end to end along the dimension named above; each array names one.
All inputs are finite; a program needn't handle non-finite values.
Results may differ from a plain program's by a relative error of at most 0.012.
Values are sent between devices in bfloat16 or wider.
A program may use at most 2 GiB of HBM per device.

v0:
```python
import jax
import jax.numpy as jnp
from jax import lax
from jax.sharding import PartitionSpec as P


def einsum(form, a, b):
    return jnp.einsum(form, a.astype(jnp.float32), b.astype(jnp.float32))


def part_of(q, k, v):
    grouped = q.reshape(q.shape[0], k.shape[2], -1, q.shape[2])
    scores = einsum("bgsd,bugd->bgsu", grouped, k) * q.shape[2] ** -0.5
    high = jnp.max(scores, -1, keepdims=True)
    weights = jnp.exp(scores - high)
    seen = einsum("bgsu,bugd->bgsd", weights.astype(jnp.bfloat16), v)
    return jnp.concatenate([seen, jnp.sum(weights, -1, keepdims=True), high], -1)


def together(parts):
    seen, total, high = parts[..., :-2], parts[..., -2:-1], parts[..., -1:]
    scale = jnp.exp(high - jnp.max(high, 0))
    return (jnp.sum(seen * scale, 0) / jnp.sum(total * scale, 0)).astype(jnp.bfloat16)


def solution(mesh):
    def step(q, k, v):
        return together(lax.all_gather(part_of(q, k, v), "sp")).reshape(q.shape)

    return jax.shard_map(
        step,
        mesh=mesh,
        in_specs=(P("dp", None, None), P("dp", "sp", None, None), P("dp", "sp", None, None)),
        out_specs=P("dp", None, None),
        check_vma=False,
    )
```

profile of v0, /device:TPU:0, one launch (start us, length us, event | category | flops | bytes accessed | tf_op | source)
XLA Modules:
  0.0 153.6 jit_solution(12243914528851997896)
XLA Ops:
  6.5 0.0 all-gather.3.cloned.1.call-start
  6.5 15.9 %fusion.7 = f32[32,32,1,256]{3,2,1,0:T(1,128)S(1)} fusion(bf16[32,256,32,80]{1,3,2,0:T(8,128)(2,1)} %param.4, bf16[32,32,80,1]{2,1,0,3:T(8,128)(2,1)} %bitcast.26), kind=kOutput, calls=%fused_computation.12 | convolution fusion | flops 41943040 | bytes 43155456 | tf_op jit(solution)/shard_map/bgsd,bugd->bgsu/dot_general | solution.py:8
  22.4 0.2 fusion.5
  22.6 0.4 fusion.6
  23.1 0.3 copy.17
  23.3 0.3 copy.16
  23.6 16.8 %fusion.1 = f32[32,32,1,80]{3,2,1,0:T(1,128)S(1)} fusion(bf16[32,256,32,80]{1,3,2,0:T(8,128)(2,1)} %param.5, bf16[32,32,256,1]{2,1,0,3:T(8,128)(2,1)S(1)} %get-tuple-element.7), kind=kOutput, calls=%fused_computation.4 | convolution fusion | flops 41943040 | bytes 42795008 | tf_op jit(solution)/shard_map/bgsu,bugd->bgsd/dot_general | solution.py:8
  40.4 1.2 pad_maximum_fusion
  41.6 0.0 all-gather.3.cloned.1.call-update
  41.6 77.4 %all-gather.3.cloned.1.call-done = f32[512,32,1,82]{3,1,2,0:T(8,128)} async-done(((f32[32,32,1,82]{3,1,2,0:T(8,128)}), f32[512,32,1,82]{3,1,2,0:T(8,128)}) %all-gather.3.cloned.1.call-update) | async-done | bytes 5373968 | tf_op jit(solution)/shard_map/all_gather | solution.py:28
  119.0 15.3 %copy.18 = f32[512,32,1,82]{1,0,3,2:T(8,128)} copy(f32[512,32,1,82]{3,1,2,0:T(8,128)} %all-gather.3.cloned.1.call-done) | data formatting | bytes 10747904 | tf_op jit(solution)/shard_map/all_gather | solution.py:28
  134.3 1.0 slice_reduce_fusion
  135.3 1.1 fusion.9
  136.4 8.8 %fusion = f32[32,32,80]{1,0,2:T(8,128)S(1)} fusion(f32[16,32,32,1,82]{2,1,0,4,3:T(8,128)} %bitcast.25, f32[16,32,32]{2,1,0:T(8,128)S(1)} %get-tuple-element.6), kind=kLoop, calls=%fused_computation.1 | loop fusion | flops 2539520 | bytes 5636096 | tf_op jit(solution)/shard_map/reduce_sum | solution.py:23
  145.2 0.1 divide_convert_fusion
  145.3 1.4 copy.19
Async XLA Ops:
  6.5 112.5 %all-gather.3.cloned.1.call-start = ((), (), s32[]{:S(2)}) async-start(), calls=%async_computation | async-start | bytes 8912896 | tf_op jit(solution)/shard_map/all_gather | solution.py:28
Sparse Core Ops, SparseCore 0:
  41.7 77.2 all-gather.2
where the time goes:
time: 154 us
  waiting for transfers between devices  77.5 us (50%)
  matrix products  32.6 us (21%)
  local copies, waits for them, and re-layouts  17.2 us (11%)
  between operations  13.4 us (9%)
  other arithmetic  12.8 us (8%)
    all_gather x1, waiting for transfers between devices, step(): return together(lax.all_gather(part_of(q, k, v), 'sp')).reshape(q.shape)  77.4 us
    dot_general x2, matrix products, einsum(): return jnp.einsum(form, a.astype(jnp.float32), b.astype(jnp.float32))  32.6 us
    all_gather x1, local copies, waits for them, and re-layouts, step(): return together(lax.all_gather(part_of(q, k, v), 'sp')).reshape(q.shape)  15.3 us
    reduce_sum x1, other arithmetic, together(): jnp.sum(seen * scale, 0) / jnp.sum(total * scale, 0)  8.78 us
  transfers between devices with their start and end apart: 1, of which 1 were waited for; matrix products, arithmetic and copies ran while one was open for 0% of the time, Pallas kernels for 0%

commit v1 on v0

v1 whole, which is shorter than its diff:
```python
import functools

import jax
import jax.numpy as jnp
from jax import lax
from jax.experimental import pallas as pl
from jax.experimental.pallas import tpu as pltpu
from jax.sharding import PartitionSpec as P

SLOTS = 8
LANES = 128


def owner_chip(b):
    return lax.rem(3 * lax.rem(b, 8) + 4, 8)


def kernel(scale, q_ref, k_hbm, v_hbm, out_ref, kbuf, vbuf, mask, qpad, turned, weights, stats, send, recv,
           ksem, vsem, rs_send, rs_recv, ag_send, ag_recv):
    batches, heads, head = q_ref.shape
    tokens = k_hbm.shape[-1]
    half = heads // 2
    n = 16
    me = lax.axis_index("sp")
    my_chip, my_core = me // 2, lax.rem(me, 2)

    def fetch(hbm, buf, sem, b):
        return pltpu.make_async_copy(hbm.at[b], buf.at[lax.rem(b, SLOTS)], sem.at[lax.rem(b, SLOTS)])

    for b in range(SLOTS):
        fetch(k_hbm, kbuf, ksem, b).start()
        fetch(v_hbm, vbuf, vsem, b).start()

    barrier = pltpu.get_barrier_semaphore()
    for d in range(1, n):
        pl.semaphore_signal(barrier, 1, device_id={"sp": lax.rem(me + d, n)}, device_id_type=pl.DeviceIdType.MESH)

    row = lax.broadcasted_iota(jnp.int32, (heads, heads * head), 0)
    col = lax.broadcasted_iota(jnp.int32, (heads, heads * head), 1)
    mask[...] = jnp.where((col >= row * head) & (col < row * head + head), 1.0, 0.0).astype(jnp.bfloat16)
    qpad[...] = jnp.zeros_like(qpad)
    lane = lax.broadcasted_iota(jnp.int32, (heads, LANES), 1)
    shift = lax.rem(lax.broadcasted_iota(jnp.int32, (heads, LANES), 0) * head, LANES)

    def turn(i, carry):
        for j in range(2):
            qpad[j, :, :head] = q_ref[2 * i + j].astype(jnp.float32)
            x = qpad[j]
            for bit in (16, 32, 64):
                x = jnp.where((shift & bit) != 0, pltpu.roll(x, bit, 1), x)
            turned[2 * i + j] = x.astype(jnp.bfloat16)
        return carry

    lax.fori_loop(0, batches // 2, turn, 0)

    def score(b):
        wide = jnp.concatenate([turned[b]] * (heads * head // LANES), axis=1) * mask[...]
        keys = kbuf[lax.rem(b, SLOTS)].reshape(heads * head, tokens)
        scores = jnp.dot(wide, keys, preferred_element_type=jnp.float32) * scale
        high = jnp.max(scores, 1, keepdims=True)
        w = jnp.exp(scores - high)
        total = jnp.sum(w, 1, keepdims=True)
        return w.astype(jnp.bfloat16), jnp.where(lane == head, high, jnp.where(lane == head + 1, total, 0.0))

    def keep(b, result):
        weights[lax.rem(b, 2)] = result[0]
        stats[lax.rem(b, 2)] = result[1]

    def gather_values(b):
        values = vbuf[lax.rem(b, SLOTS)].reshape(heads * head, tokens)
        every = lax.dot_general(values, weights[lax.rem(b, 2)], (((1,), (1,)), ((), ())),
                                preferred_element_type=jnp.float32)
        which = lax.broadcasted_iota(jnp.int32, (head, heads), 1)
        own = jnp.zeros((head, heads), jnp.float32)
        for h in range(heads):
            own = jnp.where(which == h, every[h * head:(h + 1) * head], own)
        return own

    def finish(b, own):
        send[b, :, :] = stats[lax.rem(b, 2)]
        send[b, :, :head] = own.T

    def scatter(b):
        chip = owner_chip(b)
        for core in range(2):
            target = 2 * chip + core

            @pl.when(target != me)
            def _():
                pltpu.make_async_remote_copy(
                    src_ref=send.at[b, pl.ds(core * half, half)],
                    dst_ref=recv.at[b // 8, lax.rem(me - target + 2 * n - 1, n)],
                    send_sem=rs_send, recv_sem=rs_recv.at[b // 8],
                    device_id={"sp": target}, device_id_type=pl.DeviceIdType.MESH,
                ).start()

    def combine(r):
        b = 8 * r + lax.rem(3 * my_chip + 4, 8)
        pltpu.make_async_copy(recv.at[r], recv.at[r], rs_recv.at[r]).wait()
        rows = pl.ds(pl.multiple_of(my_core * half, half), half)
        mine = send[b, rows, :]
        parts = [mine] + [recv[r, i] for i in range(n - 1)]
        highs = [p[:, head:head + 1] for p in parts]
        high = functools.reduce(jnp.maximum, highs)
        seen = jnp.zeros_like(mine)
        for p, h in zip(parts, highs):
            seen += p * jnp.exp(h - high)
        result = seen[:, :head] / seen[:, head + 1:head + 2]
        out_ref[b, rows, :] = result.astype(out_ref.dtype)
        for d in range(1, n):
            pltpu.make_async_remote_copy(
                src_ref=out_ref.at[b, rows], dst_ref=out_ref.at[b, rows],
                send_sem=ag_send, recv_sem=ag_recv,
                device_id={"sp": lax.rem(me + d, n)}, device_id_type=pl.DeviceIdType.MESH,
            ).start()

    fetch(k_hbm, kbuf, ksem, 0).wait()
    keep(0, score(0))
    pl.semaphore_wait(barrier, n - 1)

    def step(s, carry):
        b = s - 1
        fetch(k_hbm, kbuf, ksem, s).wait()
        fetch(v_hbm, vbuf, vsem, b).wait()
        result = score(s)
        own = gather_values(b)
        keep(s, result)
        finish(b, own)

        @pl.when(b + SLOTS < batches)
        def _():
            fetch(k_hbm, kbuf, ksem, b + SLOTS).start()
            fetch(v_hbm, vbuf, vsem, b + SLOTS).start()

        scatter(b)

        @pl.when((b >= 8) & (owner_chip(b) == my_chip))
        def _():
            combine(b // 8 - 1)

        return carry

    lax.fori_loop(1, batches, step, 0)
    last = batches - 1
    fetch(v_hbm, vbuf, vsem, last).wait()
    finish(last, gather_values(last))
    scatter(last)

    @pl.when(owner_chip(last) == my_chip)
    def _():
        combine(batches // 8 - 2)

    combine(batches // 8 - 1)
    pltpu.make_async_copy(recv, recv, rs_send).wait()
    sent = out_ref.at[pl.ds(0, batches // 16 * (n - 1))]
    pltpu.make_async_copy(sent, sent, ag_recv).wait()
    pltpu.make_async_copy(sent, sent, ag_send).wait()


def attend(q, k, v):
    batches, tokens, heads, head = k.shape
    n = 16
    return pl.pallas_call(
        functools.partial(kernel, head ** -0.5),
        out_shape=jax.ShapeDtypeStruct(q.shape, jnp.bfloat16),
        in_specs=[pl.BlockSpec(memory_space=pltpu.VMEM), pl.BlockSpec(memory_space=pl.ANY),
                  pl.BlockSpec(memory_space=pl.ANY)],
        out_specs=pl.BlockSpec(memory_space=pltpu.VMEM),
        scratch_shapes=[
            pltpu.VMEM((SLOTS, heads, head, tokens), jnp.bfloat16),
            pltpu.VMEM((SLOTS, heads, head, tokens), jnp.bfloat16),
            pltpu.VMEM((heads, heads * head), jnp.bfloat16),
            pltpu.VMEM((2, heads, LANES), jnp.float32),
            pltpu.VMEM((batches, heads, LANES), jnp.bfloat16),
            pltpu.VMEM((2, heads, tokens), jnp.bfloat16),
            pltpu.VMEM((2, heads, LANES), jnp.float32),
            pltpu.VMEM((batches, heads, LANES), jnp.float32),
            pltpu.VMEM((batches // 8, n - 1, heads // 2, LANES), jnp.float32),
            pltpu.SemaphoreType.DMA((SLOTS,)),
            pltpu.SemaphoreType.DMA((SLOTS,)),
            pltpu.SemaphoreType.DMA,
            pltpu.SemaphoreType.DMA((batches // 8,)),
            pltpu.SemaphoreType.DMA,
            pltpu.SemaphoreType.DMA,
        ],
        compiler_params=pltpu.CompilerParams(collective_id=0, has_side_effects=True, vmem_limit_bytes=60 * 2**20),
    )(q, jnp.transpose(k, (0, 2, 3, 1)), jnp.transpose(v, (0, 2, 3, 1)))


def solution(mesh):
    return jax.shard_map(
        attend,
        mesh=mesh,
        in_specs=(P("dp", None, None), P("dp", "sp", None, None), P("dp", "sp", None, None)),
        out_specs=P("dp", None, None),
        check_vma=False,
    )
```

time: 154 us -> 42.2 us (0.27)
  waiting for transfers between devices: 77.5 us -> 0 us
  Pallas kernels: 0 us -> 40.3 us
  matrix products: 32.6 us -> 0 us
  local copies, waits for them, and re-layouts: 17.2 us -> 1.67 us
  between operations: 13.4 us -> 0.01 us
  other arithmetic: 12.8 us -> 0 us
    all_gather x1 -> x0, waiting for transfers between devices: 77.4 us -> none  [step(): return together(lax.all_gather(part_of(q, k, v), 'sp')).reshape(q.shape)]
    pallas_call x0 -> x1, Pallas kernels: none -> 40.3 us  [attend(): pl.pallas_call(functools.partial(kernel, head ** (-0.5)), out_shape=jax.S...]
    dot_general x2 -> x0, matrix products: 32.6 us -> none  [einsum(): return jnp.einsum(form, a.astype(jnp.float32), b.astype(jnp.float32))]
    all_gather x1 -> x0, local copies, waits for them, and re-layouts: 15.3 us -> none  [step(): return together(lax.all_gather(part_of(q, k, v), 'sp')).reshape(q.shape)]
    reduce_sum x2 -> x0, other arithmetic: 9.87 us -> none  [the longest x1 8.78 us: together(): jnp.sum(seen * scale, 0) / jnp.sum(total * scale, 0)]
    unnamed x0 -> x1, local copies, waits for them, and re-layouts: none -> 1.67 us
  transfers between devices with their start and end apart: 1 -> 0, of which waited for: 1 -> 0; matrix products, arithmetic and copies ran while one was open for 0% -> 0% of each run, Pallas kernels for 0% -> 0%
where the time goes in v1:
time: 42.2 us; the launch traced here: 42 us
  Pallas kernels  40.3 us (95%)
  local copies, waits for them, and re-layouts  1.67 us (4%)
    pallas_call x1, Pallas kernels, attend(): pl.pallas_call(functools.partial(kernel, head ** (-0.5)), out_shape=jax.S...  40.3 us
    unnamed x1, local copies, waits for them, and re-layouts  1.67 us

profile of v1, /device:TPU:0, one launch (start us, length us, event | category | flops | bytes accessed | tf_op | source)
XLA Modules:
  0.0 42.0 jit_solution(2511637969837913095)
XLA Ops:
  0.0 40.3 %shard_map.37 = bf16[32,32,80]{2,1,0:T(8,128)(2,1)} custom-call(bf16[32,32,80]{2,1,0:T(8,128)(2,1)} %q_ref.1, bf16[32,32,80,256]{3,2,1,0:T(8,128)(2,1)} %bitcast.2, bf16[32,32,80,256]{3,2,1,0:T(8,128)(2,1)} %bitcast.3), custom_call_target="tpu_custom_call" | custom-call | tf_op jit(solution)/shard_map/pallas_call | solution.py:163
  40.3 1.7 %copy.5 = bf16[32,32,80]{2,1,0:T(8,128)(2,1)} copy(bf16[32,32,80]{2,1,0:T(8,128)(2,1)} %shard_map.37) | data formatting | bytes 327680

commit v2 on v0

v2 whole, which is shorter than its diff:
```python
import functools

import jax
import jax.numpy as jnp
from jax import lax
from jax.experimental import pallas as pl
from jax.experimental.pallas import tpu as pltpu
from jax.sharding import PartitionSpec as P

SLOTS = 8
LAG = 5
LANES = 128
N = 16
GROUPS = 2


def chip_of(i):
    inner, t = i // 4, lax.rem(i, 2)
    return lax.rem(i, 4) // 2 * 4 + inner * (1 + t) + (1 - inner) * 3 * t


def batch_of(chip):
    y, z = chip // 4, lax.rem(chip, 4)
    inner = z * (3 - z) // 2
    return 4 * inner + 2 * y + inner * (z - 1) + (1 - inner) * (z // 3)


def kernel(scale, q_hbm, k_hbm, v_hbm, out_ref, q_ref, kbuf, vbuf, mask, qpad, turned, weights, stats, send, recv,
           qsem, ksem, vsem, part_send_sem, part_sem, out_send_sem, out_sem):
    batches, heads, head = q_ref.shape
    tokens = k_hbm.shape[-1]
    half = heads // 2
    run = heads // GROUPS
    rounds = batches // 8
    me = lax.axis_index("sp")
    my_batch, my_core = batch_of(me // 2), lax.rem(me, 2)

    def fetch(hbm, buf, sem, b):
        return pltpu.make_async_copy(hbm.at[b], buf.at[lax.rem(b, SLOTS)], sem.at[lax.rem(b, SLOTS)])

    def give(src, dst, send_sem, recv_sem, target):
        return pltpu.make_async_remote_copy(src_ref=src, dst_ref=dst, send_sem=send_sem, recv_sem=recv_sem,
                                            device_id={"sp": target}, device_id_type=pl.DeviceIdType.MESH)

    q_copy = pltpu.make_async_copy(q_hbm, q_ref, qsem)
    fetch(k_hbm, kbuf, ksem, 0).start()
    q_copy.start()
    for b in range(SLOTS):
        if b:
            fetch(k_hbm, kbuf, ksem, b).start(priority=1)
        fetch(v_hbm, vbuf, vsem, b).start(priority=1)

    barrier = pltpu.get_barrier_semaphore()
    for d in range(1, N):
        pl.semaphore_signal(barrier, 1, device_id={"sp": lax.rem(me + d, N)}, device_id_type=pl.DeviceIdType.MESH)

    row = lax.broadcasted_iota(jnp.int32, (run, run * head), 0) * head
    col = lax.broadcasted_iota(jnp.int32, (run, run * head), 1)
    mask[...] = jnp.where((col >= row) & (col < row + head), 1.0, 0.0).astype(jnp.bfloat16)
    qpad[...] = jnp.zeros_like(qpad)
    lane = lax.broadcasted_iota(jnp.int32, (run, LANES), 1)
    which = lax.broadcasted_iota(jnp.int32, (head, run), 1)
    shift = lax.rem(lax.broadcasted_iota(jnp.int32, (heads, LANES), 0) * head, LANES)

    def turn(b, i):
        qpad[i, :, :head] = q_ref[jnp.minimum(b, batches - 1)].astype(jnp.float32)
        x = qpad[i]
        for bit in (16, 32, 64):
            x = jnp.where((shift & bit) != 0, pltpu.roll(x, bit, 1), x)
        turned[i] = x.astype(jnp.bfloat16)

    def score(b, queries):
        weights, stats = [], []
        for g in range(GROUPS):
            wide = jnp.concatenate([queries[g * run:(g + 1) * run]] * (run * head // LANES), axis=1) * mask[...]
            keys = kbuf[lax.rem(b, SLOTS), g * run:(g + 1) * run].reshape(run * head, tokens)
            scores = jnp.dot(wide, keys, preferred_element_type=jnp.float32) * scale
            high = jnp.max(scores, 1, keepdims=True)
            w = jnp.exp(scores - high)
            total = jnp.sum(w, 1, keepdims=True)
            weights.append(w.astype(jnp.bfloat16))
            stats.append(jnp.where(lane == head, high, jnp.where(lane == head + 1, total, 0.0)))
        return weights, stats

    def see(b, weights):
        sums = []
        for g in range(GROUPS):
            values = vbuf[lax.rem(b, SLOTS), g * run:(g + 1) * run].reshape(run * head, tokens)
            every = lax.dot_general(values, weights[g], (((1,), (1,)), ((), ())), preferred_element_type=jnp.float32)
            own = jnp.zeros((head, run), jnp.float32)
            for h in range(run):
                own = jnp.where(which == h, every[h * head:(h + 1) * head], own)
            sums.append(own.T)
        return sums

    def part(b, sums, stats):
        for g in range(GROUPS):
            send[b, g * run:(g + 1) * run, :] = stats[g]
            send[b, g * run:(g + 1) * run, :head] = sums[g]

    def keep(new):
        for g in range(GROUPS):
            weights[g], stats[g] = new[0][g], new[1][g]

    def kept():
        return [weights[g] for g in range(GROUPS)], [stats[g] for g in range(GROUPS)]

    def scatter(b):
        for core in range(2):
            target = 2 * chip_of(lax.rem(b, 8)) + core

            @pl.when(target != me)
            def _():
                give(send.at[b, pl.ds(core * half, half)], recv.at[b // 8, lax.rem(me - target + 2 * N - 1, N)],
                     part_send_sem, part_sem.at[b // 8], target).start()

    def combine(r):
        b = 8 * r + my_batch
        pltpu.make_async_copy(recv.at[r], recv.at[r], part_sem.at[r]).wait()
        rows = pl.ds(pl.multiple_of(my_core * half, half), half)
        parts = [send[b, rows, :]] + [recv[r, i] for i in range(N - 1)]
        highs = [p[:, head:head + 1] for p in parts]
        high = functools.reduce(jnp.maximum, highs)
        seen = functools.reduce(jnp.add, [p * jnp.exp(h - high) for p, h in zip(parts, highs)])
        out_ref[b, rows, :] = (seen[:, :head] / seen[:, head + 1:head + 2]).astype(out_ref.dtype)
        for d in range(1, N):
            give(out_ref.at[b, rows], out_ref.at[b, rows], out_send_sem, out_sem, lax.rem(me + d, N)).start()

    q_copy.wait()
    turn(0, 0)
    first = turned[0]
    turn(1, 0)
    turn(2, 1)
    fetch(k_hbm, kbuf, ksem, 0).wait()
    keep(score(0, first))

    def step(i, carry):
        b = 2 * i
        fetch(k_hbm, kbuf, ksem, b + 1).wait()
        fetch(v_hbm, vbuf, vsem, b).wait()
        fetch(k_hbm, kbuf, ksem, b + 2).wait()
        fetch(v_hbm, vbuf, vsem, b + 1).wait()
        w0, s0 = kept()
        queries = [turned[0], turned[1]]
        w1, s1 = score(b + 1, queries[0])
        r0 = see(b, w0)
        new = score(b + 2, queries[1])
        r1 = see(b + 1, w1)
        turn(b + 3, 0)
        turn(b + 4, 1)
        part(b, r0, s0)
        part(b + 1, r1, s1)
        keep(new)

        for j in range(2):
            @pl.when(b + j + 1 + SLOTS < batches)
            def _():
                fetch(k_hbm, kbuf, ksem, b + j + 1 + SLOTS).start(priority=1)

            @pl.when(b + j + SLOTS < batches)
            def _():
                fetch(v_hbm, vbuf, vsem, b + j + SLOTS).start(priority=1)

        @pl.when(i == 0)
        def _():
            pl.semaphore_wait(barrier, N - 1)

        scatter(b)
        scatter(b + 1)

        for j in range(2):
            @pl.when((i >= LAG) & (lax.rem(b + j - 2 * LAG + 8, 8) == my_batch))
            def _():
                combine((b + j - 2 * LAG) // 8)

        return carry

    fetch(k_hbm, kbuf, ksem, SLOTS).start()
    lax.fori_loop(0, batches // 2 - 1, step, 0)
    last = batches - 1
    fetch(k_hbm, kbuf, ksem, last).wait()
    fetch(v_hbm, vbuf, vsem, last - 1).wait()
    w0, s0 = kept()
    w1, s1 = score(last, turned[0])
    part(last - 1, see(last - 1, w0), s0)
    scatter(last - 1)
    fetch(v_hbm, vbuf, vsem, last).wait()
    part(last, see(last, w1), s1)
    scatter(last)

    @pl.when(batches - 16 + my_batch >= batches - 2 * LAG - 2)
    def _():
        combine(rounds - 2)

    combine(rounds - 1)

    pltpu.make_async_copy(recv, recv, part_send_sem).wait()
    sent = out_ref.at[pl.ds(0, rounds * (N - 1) // 2)]
    pltpu.make_async_copy(sent, sent, out_sem).wait()
    pltpu.make_async_copy(sent, sent, out_send_sem).wait()


def attend(q, k, v):
    batches, tokens, heads, head = k.shape
    run = heads // GROUPS
    return pl.pallas_call(
        functools.partial(kernel, head ** -0.5),
        out_shape=jax.ShapeDtypeStruct(q.shape, jnp.bfloat16),
        in_specs=[pl.BlockSpec(memory_space=pltpu.HBM)] * 3,
        out_specs=pl.BlockSpec(memory_space=pltpu.VMEM),
        scratch_shapes=[
            pltpu.VMEM(q.shape, jnp.bfloat16),
            pltpu.VMEM((SLOTS, heads, head, tokens), jnp.bfloat16),
            pltpu.VMEM((SLOTS, heads, head, tokens), jnp.bfloat16),
            pltpu.VMEM((run, run * head), jnp.bfloat16),
            pltpu.VMEM((2, heads, LANES), jnp.float32),
            pltpu.VMEM((2, heads, LANES), jnp.bfloat16),
            pltpu.VMEM((GROUPS, run, tokens), jnp.bfloat16),
            pltpu.VMEM((GROUPS, run, LANES), jnp.float32),
            pltpu.VMEM((batches, heads, LANES), jnp.float32),
            pltpu.VMEM((batches // 8, N - 1, heads // 2, LANES), jnp.float32),
            pltpu.SemaphoreType.DMA,
            pltpu.SemaphoreType.DMA((SLOTS,)),
            pltpu.SemaphoreType.DMA((SLOTS,)),
            pltpu.SemaphoreType.DMA,
            pltpu.SemaphoreType.DMA((batches // 8,)),
            pltpu.SemaphoreType.DMA,
            pltpu.SemaphoreType.DMA,
        ],
        compiler_params=pltpu.CompilerParams(collective_id=0, has_side_effects=True, vmem_limit_bytes=30 * 2**20),
    )(pltpu.with_memory_space_constraint(q, pltpu.HBM), jnp.transpose(k, (0, 2, 3, 1)), jnp.transpose(v, (0, 2, 3, 1)))


def solution(mesh):
    return jax.shard_map(
        attend,
        mesh=mesh,
        in_specs=(P("dp", None, None), P("dp", "sp", None, None), P("dp", "sp", None, None)),
        out_specs=P("dp", None, None),
        check_vma=False,
    )
```

time: 154 us -> 38.4 us (0.25)
  waiting for transfers between devices: 77.5 us -> 0 us
  Pallas kernels: 0 us -> 37.5 us
  matrix products: 32.6 us -> 0 us
  local copies, waits for them, and re-layouts: 17.2 us -> 0.71 us
  between operations: 13.4 us -> 0.01 us
  other arithmetic: 12.8 us -> 0 us
    all_gather x1 -> x0, waiting for transfers between devices: 77.4 us -> none  [step(): return together(lax.all_gather(part_of(q, k, v), 'sp')).reshape(q.shape)]
    pallas_call x0 -> x1, Pallas kernels: none -> 37.5 us  [attend(): pl.pallas_call(functools.partial(kernel, head ** (-0.5)), out_shape=jax.S...]
    dot_general x2 -> x0, matrix products: 32.6 us -> none  [einsum(): return jnp.einsum(form, a.astype(jnp.float32), b.astype(jnp.float32))]
    all_gather x1 -> x0, local copies, waits for them, and re-layouts: 15.3 us -> none  [step(): return together(lax.all_gather(part_of(q, k, v), 'sp')).reshape(q.shape)]
    reduce_sum x2 -> x0, other arithmetic: 9.87 us -> none  [the longest x1 8.78 us: together(): jnp.sum(seen * scale, 0) / jnp.sum(total * scale, 0)]
  transfers between devices with their start and end apart: 1 -> 0, of which waited for: 1 -> 0; matrix products, arithmetic and copies ran while one was open for 0% -> 0% of each run, Pallas kernels for 0% -> 0%
where the time goes in v2:
time: 38.4 us; the launch traced here: 38.2 us
  Pallas kernels  37.5 us (98%)
  local copies, waits for them, and re-layouts  0.71 us (2%)
    pallas_call x1, Pallas kernels, attend(): pl.pallas_call(functools.partial(kernel, head ** (-0.5)), out_shape=jax.S...  37.5 us

profile of v2, /device:TPU:0, one launch (start us, length us, event | category | flops | bytes accessed | tf_op | source)
XLA Modules:
  0.0 38.2 jit_solution(18391992425732848617)
XLA Ops:
  0.0 37.5 %shard_map.37 = bf16[32,32,80]{2,1,0:T(8,128)(2,1)S(1)} custom-call(bf16[32,32,80]{2,1,0:T(8,128)(2,1)} %q_hbm.1, bf16[32,32,80,256]{3,2,1,0:T(8,128)(2,1)} %bitcast.2, bf16[32,32,80,256]{3,2,1,0:T(8,128)(2,1)} %bitcast.3), custom_call_target="tpu_custom_call" | custom-call | tf_op jit(solution)/shard_map/pallas_call | solution.py:206
  37.5 0.7 %copy.5 = bf16[32,32,80]{2,1,0:T(8,128)(2,1)} copy(bf16[32,32,80]{2,1,0:T(8,128)(2,1)S(1)} %shard_map.37) | data formatting | bytes 327680

commit v3 on v2

--- a/solution.py
+++ b/solution.py
@@ -8,21 +8,23 @@
 from jax.sharding import PartitionSpec as P
 
 SLOTS = 8
-LAG = 5
+LAG = 4
 LANES = 128
 N = 16
 GROUPS = 2
-
-
-def chip_of(i):
-    inner, t = i // 4, lax.rem(i, 2)
-    return lax.rem(i, 4) // 2 * 4 + inner * (1 + t) + (1 - inner) * 3 * t
-
-
-def batch_of(chip):
-    y, z = chip // 4, lax.rem(chip, 4)
-    inner = z * (3 - z) // 2
-    return 4 * inner + 2 * y + inner * (z - 1) + (1 - inner) * (z // 3)
+TAIL = 2
+
+
+def owner_of(b, half):
+    high, low = lax.rem(b, 4) // 2, lax.rem(b, 2)
+    z = (1 - high) * (3 - low) + high * low
+    return (4 * half + z) * 2 + lax.rem(b // 4, 2)
+
+
+def batch_of(device):
+    z, core = lax.rem(device // 2, 4), lax.rem(device, 2)
+    back = z // 2
+    return 4 * core + 2 * (1 - back) + back * (3 - z) + (1 - back) * z
 
 
 def kernel(scale, q_hbm, k_hbm, v_hbm, out_ref, q_ref, kbuf, vbuf, mask, qpad, turned, weights, stats, send, recv,
@@ -33,7 +35,8 @@
     run = heads // GROUPS
     rounds = batches // 8
     me = lax.axis_index("sp")
-    my_batch, my_core = batch_of(me // 2), lax.rem(me, 2)
+    my_batch = batch_of(me)
+    mine = pl.ds(pl.multiple_of(me // 8 * half, half), half)
 
     def fetch(hbm, buf, sem, b):
         return pltpu.make_async_copy(hbm.at[b], buf.at[lax.rem(b, SLOTS)], sem.at[lax.rem(b, SLOTS)])
@@ -98,97 +101,107 @@
             send[b, g * run:(g + 1) * run, :] = stats[g]
             send[b, g * run:(g + 1) * run, :head] = sums[g]
 
-    def keep(new):
-        for g in range(GROUPS):
-            weights[g], stats[g] = new[0][g], new[1][g]
-
-    def kept():
-        return [weights[g] for g in range(GROUPS)], [stats[g] for g in range(GROUPS)]
+    def keep(i, new):
+        for g in range(GROUPS):
+            weights[i, g], stats[i, g] = new[0][g], new[1][g]
+
+    def kept(i):
+        return [weights[i, g] for g in range(GROUPS)], [stats[i, g] for g in range(GROUPS)]
 
     def scatter(b):
-        for core in range(2):
-            target = 2 * chip_of(lax.rem(b, 8)) + core
+        for h in range(2):
+            target = owner_of(b, h)
 
             @pl.when(target != me)
             def _():
-                give(send.at[b, pl.ds(core * half, half)], recv.at[b // 8, lax.rem(me - target + 2 * N - 1, N)],
+                give(send.at[b, pl.ds(h * half, half)], recv.at[b // 8, lax.rem(me - target + 2 * N - 1, N)],
                      part_send_sem, part_sem.at[b // 8], target).start()
 
     def combine(r):
         b = 8 * r + my_batch
         pltpu.make_async_copy(recv.at[r], recv.at[r], part_sem.at[r]).wait()
-        rows = pl.ds(pl.multiple_of(my_core * half, half), half)
-        parts = [send[b, rows, :]] + [recv[r, i] for i in range(N - 1)]
+        parts = [send[b, mine, :]] + [recv[r, i] for i in range(N - 1)]
         highs = [p[:, head:head + 1] for p in parts]
         high = functools.reduce(jnp.maximum, highs)
         seen = functools.reduce(jnp.add, [p * jnp.exp(h - high) for p, h in zip(parts, highs)])
-        out_ref[b, rows, :] = (seen[:, :head] / seen[:, head + 1:head + 2]).astype(out_ref.dtype)
+        out_ref[b, mine, :] = (seen[:, :head] / seen[:, head + 1:head + 2]).astype(out_ref.dtype)
         for d in range(1, N):
-            give(out_ref.at[b, rows], out_ref.at[b, rows], out_send_sem, out_sem, lax.rem(me + d, N)).start()
+            give(out_ref.at[b, mine], out_ref.at[b, mine], out_send_sem, out_sem, lax.rem(me + d, N)).start()
 
     q_copy.wait()
     turn(0, 0)
-    first = turned[0]
-    turn(1, 0)
-    turn(2, 1)
-    fetch(k_hbm, kbuf, ksem, 0).wait()
-    keep(score(0, first))
+    turn(1, 1)
+    for b in range(2):
+        fetch(k_hbm, kbuf, ksem, b).wait()
+    queries = [turned[0], turned[1]]
+    turn(2, 0)
+    turn(3, 1)
+    for b in range(2):
+        keep(b, score(b, queries[b]))
+    for b in range(2):
+        fetch(k_hbm, kbuf, ksem, SLOTS + b).start(priority=1)
+
+    def work(b, count):
+        for j in range(count):
+            fetch(k_hbm, kbuf, ksem, b + 2 + j).wait()
+            fetch(v_hbm, vbuf, vsem, b + j).wait()
+        slots = [lax.rem(b + j, 2) for j in range(count)]
+        old = [kept(i) for i in slots]
+        queries = [turned[i] for i in slots]
+        new, sums = [], []
+        for j in range(count):
+            new.append(score(b + 2 + j, queries[j]))
+            sums.append(see(b + j, old[j][0]))
+        for j in range(count):
+            turn(b + 4 + j, slots[j])
+            part(b + j, sums[j], old[j][1])
+            keep(slots[j], new[j])
+
+    def exchange(b, count):
+        for j in range(count):
+            scatter(b + j)
+        for j in range(count):
+            @pl.when((b >= 2 * LAG) & (lax.rem(b + j - 2 * LAG + 8, 8) == my_batch))
+            def _():
+                combine((b + j - 2 * LAG) // 8)
 
     def step(i, carry):
         b = 2 * i
-        fetch(k_hbm, kbuf, ksem, b + 1).wait()
-        fetch(v_hbm, vbuf, vsem, b).wait()
-        fetch(k_hbm, kbuf, ksem, b + 2).wait()
-        fetch(v_hbm, vbuf, vsem, b + 1).wait()
-        w0, s0 = kept()
-        queries = [turned[0], turned[1]]
-        w1, s1 = score(b + 1, queries[0])
-        r0 = see(b, w0)
-        new = score(b + 2, queries[1])
-        r1 = see(b + 1, w1)
-        turn(b + 3, 0)
-        turn(b + 4, 1)
-        part(b, r0, s0)
-        part(b + 1, r1, s1)
-        keep(new)
-
-        for j in range(2):
-            @pl.when(b + j + 1 + SLOTS < batches)
-            def _():
-                fetch(k_hbm, kbuf, ksem, b + j + 1 + SLOTS).start(priority=1)
-
-            @pl.when(b + j + SLOTS < batches)
-            def _():
+        work(b, 2)
+
+        @pl.when(b + 2 + SLOTS < batches)
+        def _():
+            for j in range(2):
+                fetch(k_hbm, kbuf, ksem, b + 2 + j + SLOTS).start(priority=1)
+                fetch(v_hbm, vbuf, vsem, b + j + SLOTS).start(priority=1)
+
+        @pl.when(b + 2 + SLOTS == batches)
+        def _():
+            for j in range(2):
                 fetch(v_hbm, vbuf, vsem, b + j + SLOTS).start(priority=1)
 
         @pl.when(i == 0)
         def _():
             pl.semaphore_wait(barrier, N - 1)
 
+        exchange(b, 2)
+        return carry
+
+    def single(b, carry):
+        work(b, 1)
+        exchange(b, 1)
+        return carry
+
+    lax.fori_loop(0, (batches - SLOTS) // 2, step, 0)
+    lax.fori_loop(batches - SLOTS, batches - TAIL, single, 0)
+
+    for b in range(batches - TAIL, batches):
+        w, st = kept(b % 2)
+        fetch(v_hbm, vbuf, vsem, b).wait()
+        part(b, see(b, w), st)
         scatter(b)
-        scatter(b + 1)
-
-        for j in range(2):
-            @pl.when((i >= LAG) & (lax.rem(b + j - 2 * LAG + 8, 8) == my_batch))
-            def _():
-                combine((b + j - 2 * LAG) // 8)
-
-        return carry
-
-    fetch(k_hbm, kbuf, ksem, SLOTS).start()
-    lax.fori_loop(0, batches // 2 - 1, step, 0)
-    last = batches - 1
-    fetch(k_hbm, kbuf, ksem, last).wait()
-    fetch(v_hbm, vbuf, vsem, last - 1).wait()
-    w0, s0 = kept()
-    w1, s1 = score(last, turned[0])
-    part(last - 1, see(last - 1, w0), s0)
-    scatter(last - 1)
-    fetch(v_hbm, vbuf, vsem, last).wait()
-    part(last, see(last, w1), s1)
-    scatter(last)
-
-    @pl.when(batches - 16 + my_batch >= batches - 2 * LAG - 2)
+
+    @pl.when(my_batch >= 8 - 2 * LAG + 8 - TAIL)
     def _():
         combine(rounds - 2)
 
@@ -215,8 +228,8 @@
             pltpu.VMEM((run, run * head), jnp.bfloat16),
             pltpu.VMEM((2, heads, LANES), jnp.float32),
             pltpu.VMEM((2, heads, LANES), jnp.bfloat16),
-            pltpu.VMEM((GROUPS, run, tokens), jnp.bfloat16),
-            pltpu.VMEM((GROUPS, run, LANES), jnp.float32),
+            pltpu.VMEM((2, GROUPS, run, tokens), jnp.bfloat16),
+            pltpu.VMEM((2, GROUPS, run, LANES), jnp.float32),
             pltpu.VMEM((batches, heads, LANES), jnp.float32),
             pltpu.VMEM((batches // 8, N - 1, heads // 2, LANES), jnp.float32),
             pltpu.SemaphoreType.DMA,

time: 38.4 us -> 37.3 us (0.971)
  Pallas kernels: 37.5 us -> 36.5 us
    pallas_call x1, Pallas kernels: 37.5 us -> 36.5 us  [attend(): pl.pallas_call(functools.partial(kernel, head ** (-0.5)), out_shape=jax.S...]
where the time goes in v3:
time: 37.3 us; the launch traced here: 37.2 us
  Pallas kernels  36.5 us (98%)
  local copies, waits for them, and re-layouts  0.71 us (2%)
    pallas_call x1, Pallas kernels, attend(): pl.pallas_call(functools.partial(kernel, head ** (-0.5)), out_shape=jax.S...  36.5 us

profile of v3, /device:TPU:0, one launch (start us, length us, event | category | flops | bytes accessed | tf_op | source)
XLA Modules:
  0.0 37.2 jit_solution(11276047132048420375)
XLA Ops:
  0.0 36.5 %shard_map.37 = bf16[32,32,80]{2,1,0:T(8,128)(2,1)S(1)} custom-call(bf16[32,32,80]{2,1,0:T(8,128)(2,1)} %q_hbm.1, bf16[32,32,80,256]{3,2,1,0:T(8,128)(2,1)} %bitcast.2, bf16[32,32,80,256]{3,2,1,0:T(8,128)(2,1)} %bitcast.3), custom_call_target="tpu_custom_call" | custom-call | tf_op jit(solution)/shard_map/pallas_call | solution.py:219
  36.5 0.7 %copy.5 = bf16[32,32,80]{2,1,0:T(8,128)(2,1)} copy(bf16[32,32,80]{2,1,0:T(8,128)(2,1)S(1)} %shard_map.37) | data formatting | bytes 327680
